TPU v7x, 32 devices: a whole 2x2x4 slice. The times are simulated.
32 devices in a mesh: groups: 2 (over y), geom: 4 (over z), design: 2 (over x), head: 2 (over core).
Axes of the slice: x: 2, y: 2, z: 4, core: 2. Of those that a mesh axis runs over, the one named last changes fastest.
Arguments:
- point_feats: bfloat16 [4, 12288, 192], P(('groups', 'design'), ('geom', 'head')), parts along dimension 0, may hold values from -6 to 6
- block_anchor: int32 [4, 96], P(('groups', 'design'), ('geom', 'head')), parts along dimension 0, may hold values from 0 to 127, as said below
- anchor_feats: bfloat16 [4, 128, 192], P(('groups', 'design'), ('geom', 'head')), parts along dimension 0, may hold values from -4 to 4
- query_feats: bfloat16 [4, 4096, 192], P(('groups', 'design'), ('geom', 'head')), parts along dimension 0, may hold values from -6 to 6
- out_grad: bfloat16 [4, 4096, 192], P(('groups', 'design'), ('geom', 'head')), parts along dimension 0, may hold values from -6 to 6
- norm_gain: float32 [192], replicated, may hold values from 0.5 to 1.5
- w_in: bfloat16 [192, 384], replicated, may hold values from -0.4375 to 0.4375
- w_out: bfloat16 [384, 192], replicated, may hold values from -0.3125 to 0.3125
- w_query: bfloat16 [192, 192], replicated, may hold values from -0.4375 to 0.4375
- w_key: bfloat16 [192, 192], replicated, may hold values from -0.4375 to 0.4375
- w_value: bfloat16 [192, 192], replicated, may hold values from -0.4375 to 0.4375
- w_proj: bfloat16 [192, 192], replicated, may hold values from -0.4375 to 0.4375
Outputs:
- attended: bfloat16 [4, 4096, 192], P(('groups', 'design'), ('geom', 'head')), parts along dimension 0
- point_grad: bfloat16 [4, 12288, 192], P(('groups', 'design'), ('geom', 'head')), parts along dimension 0
- grad_in: float32 [384, 384], P('groups'), parts along dimension 0
- grad_out: float32 [768, 192], P('groups'), parts along dimension 0
- grad_query: float32 [384, 192], P('groups'), parts along dimension 0
- grad_key: float32 [384, 192], P('groups'), parts along dimension 0
- grad_value: float32 [384, 192], P('groups'), parts along dimension 0
- grad_proj: float32 [384, 192], P('groups'), parts along dimension 0
- grad_gain: float32 [384], P('groups'), parts along dimension 0
There are 2 independent parts, one for each index of `groups`. A program takes and returns all parts, laid end to end along the dimension named above; an argument that names none is the same for every part. Nothing has to cross between parts.
Inputs may be any that keep to these rules, and one draw needn't show every extreme that they name: `block_anchor`: block index // 12 is the device that holds the block. Each device assigns at most 2 of its blocks to anchors of any one owner (anchor // 16); in every design one owner gets exactly 2 blocks from every device.
All inputs are finite; a program needn't handle non-finite values.
Results may differ from a plain program's by a relative error of at most 0.03.
Values may be sent and summed in bfloat16 or wider, within the bound.
No kernel may reach another device: no remote copies, remote signals or barrier semaphores. Data moves between devices by JAX's collectives and lax.ppermute only.
A program may use at most 64 MiB of HBM per device.

v0:
```python
import jax
import jax.numpy as jnp
from jax import lax
from jax.sharding import PartitionSpec as P

HEADS = 3
CAP = 2


def gelu_tanh(values):
    return jax.nn.gelu(values, approximate=True)


def contract_rows(first_arg, second_arg, precision=None):
    return lax.dot_general(
        first_arg,
        second_arg,
        (((0,), (0,)), ((), ())),
        precision=precision,
        preferred_element_type=jnp.float32,
    )


def times_transposed(first_arg, second_arg):
    return lax.dot_general(
        first_arg, second_arg, (((1,), (1,)), ((), ())), preferred_element_type=jnp.float32
    )


def head_split(matrix):
    return matrix.reshape(matrix.shape[0], HEADS, matrix.shape[1] // HEADS)


def on_device(
    point_feats,
    block_anchor,
    anchor_feats,
    query_feats,
    out_grad,
    norm_gain,
    w_in,
    w_out,
    w_query,
    w_key,
    w_value,
    w_proj,
):
    exact_mode = lax.Precision.HIGHEST
    owners = lax.axis_size(("geom", "head"))
    points = point_feats[0]
    assigned = block_anchor[0]
    anchor_rows = anchor_feats[0]
    query_rows = query_feats[0]
    cotangent = out_grad[0]
    blocks = assigned.shape[0]
    feature_width = points.shape[1]
    hidden_width = w_in.shape[1]
    anchors_here = anchor_rows.shape[0]
    block_size = points.shape[0] // blocks
    slot_count = owners * CAP
    target = assigned // anchors_here
    within = assigned - target * anchors_here
    block_order = jnp.arange(blocks)
    earlier = (target[None, :] == target[:, None]) & (block_order[None, :] < block_order[:, None])
    slot_of = target * CAP + jnp.sum(earlier.astype(jnp.int32), axis=1)
    selector = jnp.arange(slot_count)[:, None] == slot_of[None, :]
    select_bf = selector.astype(jnp.bfloat16)
    slot_anchor = jnp.sum(jnp.where(selector, within[None, :] + 1, 0), axis=1) - 1
    pre_act = jnp.dot(points, w_in, preferred_element_type=jnp.float32)
    hidden = gelu_tanh(pre_act).astype(jnp.bfloat16)
    message = jnp.dot(hidden, w_out, preferred_element_type=jnp.float32)
    block_sums = message.reshape(blocks, block_size, feature_width).sum(axis=1)
    outgoing_sums = jnp.dot(selector.astype(jnp.float32), block_sums, precision=exact_mode)
    arrived_sums, arrived_ids = (
        lax.all_to_all(
            outgoing_sums.reshape(owners, CAP, feature_width).astype(jnp.bfloat16),
            ("geom", "head"),
            split_axis=0,
            concat_axis=0,
            tiled=True,
        ).astype(jnp.float32),
        lax.all_to_all(
            slot_anchor.astype(jnp.float32).reshape(owners, CAP).astype(jnp.bfloat16),
            ("geom", "head"),
            split_axis=0,
            concat_axis=0,
            tiled=True,
        ).astype(jnp.float32),
    )
    slot_sums = arrived_sums.reshape(slot_count, feature_width)
    slot_ids = arrived_ids.reshape(slot_count).astype(jnp.int32)
    member = (jnp.arange(anchors_here)[:, None] == slot_ids[None, :]).astype(jnp.float32)
    pooled = jnp.dot(member, slot_sums, precision=exact_mode)
    divisor = jnp.maximum(jnp.sum(member, axis=1) * block_size, 1.0)
    anchor_sum = anchor_rows.astype(jnp.float32) + pooled / divisor[:, None]
    inv_rms = lax.rsqrt(jnp.mean(anchor_sum * anchor_sum, axis=1, keepdims=True) + 1e-06)
    normed = (anchor_sum * inv_rms * norm_gain).astype(jnp.bfloat16)
    key_local = jnp.dot(normed, w_key, preferred_element_type=jnp.float32).astype(jnp.bfloat16)
    value_local = jnp.dot(normed, w_value, preferred_element_type=jnp.float32).astype(jnp.bfloat16)
    all_keys, all_values = (
        lax.all_gather(key_local, ("geom", "head"), axis=0, tiled=True),
        lax.all_gather(value_local, ("geom", "head"), axis=0, tiled=True),
    )
    query_proj = jnp.dot(query_rows, w_query, preferred_element_type=jnp.float32).astype(
        jnp.bfloat16
    )
    score_scale = 1.0 / (feature_width // HEADS) ** 0.5
    query_heads = head_split(query_proj)
    key_heads = head_split(all_keys)
    value_heads = head_split(all_values)
    scores = (
        jnp.einsum("qhd,khd->hqk", query_heads, key_heads, preferred_element_type=jnp.float32)
        * score_scale
    )
    softmax_w = jax.nn.softmax(scores, axis=-1)
    softmax_bf = softmax_w.astype(jnp.bfloat16)
    mixed_heads = (
        jnp.einsum("hqk,khd->qhd", softmax_bf, value_heads, preferred_element_type=jnp.float32)
        .reshape(-1, feature_width)
        .astype(jnp.bfloat16)
    )
    attended = jnp.dot(mixed_heads, w_proj, preferred_element_type=jnp.float32).astype(jnp.bfloat16)
    grad_proj = contract_rows(mixed_heads, cotangent)
    d_mixed = times_transposed(cotangent, w_proj).astype(jnp.bfloat16)
    dmix_heads = head_split(d_mixed)
    d_probs = jnp.einsum(
        "qhd,khd->hqk", dmix_heads, value_heads, preferred_element_type=jnp.float32
    )
    d_scores = (
        softmax_w * (d_probs - jnp.sum(softmax_w * d_probs, axis=-1, keepdims=True)) * score_scale
    ).astype(jnp.bfloat16)
    d_query = (
        jnp.einsum("hqk,khd->qhd", d_scores, key_heads, preferred_element_type=jnp.float32)
        .reshape(-1, feature_width)
        .astype(jnp.bfloat16)
    )
    key_terms = jnp.einsum(
        "hqk,qhd->khd", d_scores, query_heads, preferred_element_type=jnp.float32
    ).reshape(-1, feature_width)
    value_terms = jnp.einsum(
        "hqk,qhd->khd", softmax_bf, dmix_heads, preferred_element_type=jnp.float32
    ).reshape(-1, feature_width)
    grad_query = contract_rows(query_rows, d_query)
    key_sum, value_sum = (
        lax.psum_scatter(
            key_terms.astype(jnp.bfloat16), ("geom", "head"), scatter_dimension=0, tiled=True
        ).astype(jnp.float32),
        lax.psum_scatter(
            value_terms.astype(jnp.bfloat16), ("geom", "head"), scatter_dimension=0, tiled=True
        ).astype(jnp.float32),
    )
    key_grad = key_sum.astype(jnp.bfloat16)
    value_grad = value_sum.astype(jnp.bfloat16)
    grad_key = contract_rows(normed, key_grad)
    grad_value = contract_rows(normed, value_grad)
    d_normed = times_transposed(key_grad, w_key) + times_transposed(value_grad, w_value)
    scaled = d_normed * norm_gain
    grad_gain = jnp.sum(d_normed * anchor_sum * inv_rms, axis=0)
    d_sum = inv_rms * scaled - anchor_sum * inv_rms**3 * jnp.mean(
        scaled * anchor_sum, axis=1, keepdims=True
    )
    d_pooled = d_sum / divisor[:, None]
    slot_grad = contract_rows(member, d_pooled, exact_mode).astype(jnp.bfloat16)
    returned_grad = lax.all_to_all(
        slot_grad.reshape(owners, CAP, feature_width),
        ("geom", "head"),
        split_axis=0,
        concat_axis=0,
        tiled=True,
    )
    block_grad = contract_rows(select_bf, returned_grad.reshape(slot_count, feature_width)).astype(
        jnp.bfloat16
    )
    d_hidden_block = times_transposed(block_grad, w_out)
    d_hidden = jnp.broadcast_to(
        d_hidden_block[:, None, :], (blocks, block_size, hidden_width)
    ).reshape(-1, hidden_width)
    unused_out, gelu_back = jax.vjp(gelu_tanh, pre_act)
    d_pre = gelu_back(d_hidden)[0].astype(jnp.bfloat16)
    hidden_sum = jnp.sum(
        hidden.reshape(blocks, block_size, hidden_width), axis=1, dtype=jnp.float32
    )
    grad_out = contract_rows(hidden_sum, block_grad.astype(jnp.float32), exact_mode)
    grad_in = contract_rows(points, d_pre)
    d_input = times_transposed(d_pre, w_in).astype(jnp.bfloat16)
    reduced = lax.psum(
        (grad_in, grad_out, grad_query, grad_key, grad_value, grad_proj, grad_gain),
        ("geom", "design", "head"),
    )
    return (
        attended[None],
        d_input[None],
        reduced[0],
        reduced[1],
        reduced[2],
        reduced[3],
        reduced[4],
        reduced[5],
        reduced[6],
    )


def solution(mesh):
    placed = (
        P(("groups", "design"), ("geom", "head"), None),
        P(("groups", "design"), ("geom", "head")),
        P(("groups", "design"), ("geom", "head"), None),
        P(("groups", "design"), ("geom", "head"), None),
        P(("groups", "design"), ("geom", "head"), None),
        P(),
        P(),
        P(),
        P(),
        P(),
        P(),
        P(),
    )
    return jax.shard_map(
        on_device,
        mesh=mesh,
        in_specs=placed,
        out_specs=(
            P(("groups", "design"), ("geom", "head"), None),
            P(("groups", "design"), ("geom", "head"), None),
            P("groups", None),
            P("groups", None),
            P("groups", None),
            P("groups", None),
            P("groups", None),
            P("groups", None),
            P("groups"),
        ),
        check_vma=False,
    )
```

profile of v0, /device:TPU:0, one launch (start us, length us, event | category | flops | bytes accessed | tf_op | source)
XLA Modules:
  0.0 259.6 jit_solution(16616870421361154867)
XLA Ops:
  7.2 0.7 and_select_fusion
  7.9 0.7 add_bitcast_fusion
  8.6 0.2 convert_reduce_fusion.2
  8.8 0.1 select_reduce_fusion
  8.9 0.7 convert_element_type.190
  9.6 6.4 %all-to-all-start = ((bf16[8,1,2]{2,1,0:T(2,128)(2,1)}), bf16[8,1,2]{2,1,0:T(2,128)(2,1)S(1)}, u32[]{:S(2)}, u32[]{:S(2)}) async-start(bf16[8,1,2]{2,1,0:T(2,128)(2,1)} %convert_element_type.190), calls=%async_computation | async-start | bytes 8192 | tf_op jit(solution)/shard_map/all_to_all | solution.py:82
  16.0 3.2 %multiply_convert_fusion = (bf16[1536,384]{1,0:T(8,128)(2,1)S(1)}, f32[1536,384]{1,0:T(8,128)}) fusion(bf16[192,384]{1,0:T(8,128)(2,1)} %param.18, bf16[1,1536,192]{1,2,0:T(8,128)(2,1)S(1)} %copy-done), kind=kOutput, calls=%fused_computation.19 | convolution fusion | flops 231800832 | bytes 4276224 | tf_op jit(solution)/shard_map/dot_general | solution.py:69
  19.2 0.8 convert_reduce_fusion
  20.0 0.6 fusion.64
  20.6 0.2 reshape.166
  20.8 0.1 copy-done.1
  20.9 1.2 convolution_convert_fusion.5
  22.1 1.2 convolution_convert_fusion.1
  23.3 0.5 reduce_sum.95
  23.8 0.2 convolution_convert_fusion.12
  23.9 0.7 copy.50
  24.6 5.1 %all-to-all-start.1 = ((bf16[8,2,192]{2,1,0:T(2,128)(2,1)}), bf16[8,2,192]{2,1,0:T(2,128)(2,1)S(1)}, u32[]{:S(2)}, u32[]{:S(2)}) async-start(bf16[8,2,192]{2,1,0:T(2,128)(2,1)} %copy.50), calls=%async_computation.1 | async-start | bytes 16384 | tf_op jit(solution)/shard_map/all_to_all | solution.py:75
  29.8 0.1 convert_element_type.158
  29.9 0.1 convert_reduce_fusion.1
  30.0 5.3 %all-to-all-done.1 = bf16[8,2,192]{2,1,0:T(2,128)(2,1)S(1)} async-done(((bf16[8,2,192]{2,1,0:T(2,128)(2,1)}), bf16[8,2,192]{2,1,0:T(2,128)(2,1)S(1)}, u32[]{:S(2)}, u32[]{:S(2)}) %all-to-all-start.1) | async-done | bytes 6176 | tf_op jit(solution)/shard_map/all_to_all | solution.py:75
  35.4 0.2 multiply_reduce_fusion.3
  35.6 0.1 multiply_convert_fusion.1
  35.7 0.1 convolution_convert_fusion.10
  35.8 0.1 convolution_convert_fusion.11
  36.0 14.0 %all_gather.6 = bf16[128,192]{1,0:T(8,128)(2,1)S(1)} all-gather(bf16[16,192]{1,0:T(8,128)(2,1)S(1)} %convolution_convert_fusion.11), channel_id=1, replica_groups=mesh['groups'=2,'geom'=4,'design'=2,'head'=2] {'geom','head'}, dimensions={0}, use_global_device_ids=true | all-gather | bytes 55296 | tf_op jit(solution)/shard_map/all_gather | solution.py:102
  50.0 0.1 copy.51
  50.1 14.0 %all_gather.7 = bf16[128,192]{1,0:T(8,128)(2,1)S(1)} all-gather(bf16[16,192]{1,0:T(8,128)(2,1)S(1)} %convolution_convert_fusion.10), channel_id=1, replica_groups=mesh['groups'=2,'geom'=4,'design'=2,'head'=2] {'geom','head'}, dimensions={0}, use_global_device_ids=true | all-gather | bytes 55296 | tf_op jit(solution)/shard_map/all_gather | solution.py:101
  64.1 0.1 copy.52
  64.2 0.3 fusion.65
  64.5 1.3 fusion.63
  65.8 1.8 convolution_convert_fusion.7
  67.6 1.8 convolution_convert_fusion.2
  69.4 0.6 convolution_convert_fusion.4
  70.0 0.9 convolution_bitcast_fusion.1
  70.9 0.7 copy.64
  71.7 0.0 reduce-scatter.9.cloned.1.call-start
  71.7 0.9 fusion.30
  72.6 0.6 convolution_convert_fusion.6
  73.2 0.7 copy.66
  74.0 26.5 %reduce-scatter.7.cloned.1.call-done = bf16[16,192]{1,0:T(8,128)(2,1)} async-done(((bf16[128,192]{1,0:T(8,128)(2,1)}), bf16[16,192]{1,0:T(8,128)(2,1)}) %reduce-scatter.7.cloned.1.call-update) | async-done | bytes 6160
  100.5 0.8 fusion.66
  101.4 30.6 %reduce-scatter.9.cloned.1.call-done = bf16[16,192]{1,0:T(8,128)(2,1)} async-done(((bf16[128,192]{1,0:T(8,128)(2,1)}), bf16[16,192]{1,0:T(8,128)(2,1)}) %reduce-scatter.9.cloned.1.call-update) | async-done | bytes 6160
  132.0 1.0 multiply_reduce_fusion.1
  133.0 0.2 convolution_convert_fusion.9
  133.2 0.6 reshape.172
  133.8 3.3 %all-to-all-start.2 = ((bf16[8,2,192]{2,1,0:T(2,128)(2,1)}), bf16[8,2,192]{2,1,0:T(2,128)(2,1)S(1)}, u32[]{:S(2)}, u32[]{:S(2)}) async-start(bf16[8,2,192]{2,1,0:T(2,128)(2,1)} %reshape.172), calls=%async_computation.2 | async-start | bytes 16384 | tf_op jit(solution)/shard_map/all_to_all | solution.py:164
  137.2 1.6 fusion.70
  138.8 1.6 fusion.69
  140.4 2.3 all-to-all-done.2
  142.7 0.2 convolution_convert_fusion.8
  142.9 0.1 fusion.67
  143.0 1.1 fusion.68
  144.1 3.2 %fusion.9 = bf16[1536,384]{1,0:T(8,128)(2,1)S(1)} fusion(f32[1536,384]{1,0:T(8,128)} %get-tuple-element.58, f32[12,384]{1,0:T(8,128)S(1)} %fusion.67), kind=kLoop, calls=%fused_computation.14 | loop fusion | flops 11796480 | bytes 3557376 | tf_op jit(solution)/shard_map/convert_element_type | solution.py:179
  147.4 1.2 convolution_bitcast_fusion
  148.6 0.9 fusion.19
  149.5 32.4 %psum.55 = f32[192]{0:T(256)} all-reduce(f32[192]{0:T(256)S(1)} %get-tuple-element.45), channel_id=1, replica_groups=mesh['groups'=2,'geom'=4,'design'=2,'head'=2] {'geom','design','head'}, use_global_device_ids=true, to_apply=%region_19.20 | all-reduce | flops 192 | bytes 1536 | tf_op jit(solution)/shard_map/psum | solution.py:186
  181.9 1.4 fusion.2
  183.3 60.8 %all-reduce.3.cloned.1.call-done = (f32[192,384]{1,0:T(8,128)}, f32[384,192]{0,1:T(8,128)}, f32[192,192]{0,1:T(8,128)}, f32[192,192]{1,0:T(8,128)}, f32[192,192]{1,0:T(8,128)}, /*index=5*/f32[192,192]{1,0:T(8,128)}) async-done(((f32[192,384]{1,0:T(8,128)}, f32[384,192]{0,1:T(8,128)}, f32[192,192]{0,1:T(8,128)}, f32[192,192]{1,0:T(8,128)}, f32[192,192]{1,0:T(8,128)}, /*index=5*/f32[192,192]{1,0:T(8,128)}), ...) | async-done | bytes 1179664 | tf_op jit(solution)/shard_map/psum | solution.py:186
  244.0 1.8 copy.57
  245.8 1.7 copy.74
  247.5 1.7 copy.75
  249.2 1.6 copy.76
  250.8 1.6 copy.77
  252.4 0.7 copy.78
  (40 shorter events, 0.3 us)
Async XLA Ops:
  7.2 8.8 %copy-start = (bf16[1,1536,192]{1,2,0:T(8,128)(2,1)S(1)}, bf16[1,1536,192]{1,2,0:T(8,128)(2,1)}, u32[]{:S(2)}) copy-start(bf16[1,1536,192]{1,2,0:T(8,128)(2,1)} %param.12) | copy-start | bytes 1769476
  9.6 15.0 %all-to-all-start = ((bf16[8,1,2]{2,1,0:T(2,128)(2,1)}), bf16[8,1,2]{2,1,0:T(2,128)(2,1)S(1)}, u32[]{:S(2)}, u32[]{:S(2)}) async-start(bf16[8,1,2]{2,1,0:T(2,128)(2,1)} %convert_element_type.190), calls=%async_computation | async-start | bytes 8192 | tf_op jit(solution)/shard_map/all_to_all | solution.py:82
  16.0 4.0 %copy-start.3 = (bf16[384,192]{0,1:T(8,128)(2,1)S(1)}, bf16[384,192]{0,1:T(8,128)(2,1)}, u32[]{:S(2)}) copy-start(bf16[384,192]{0,1:T(8,128)(2,1)} %param.19) | copy-start | bytes 442372
  20.0 0.9 copy-start.1
  20.6 15.0 %copy-start.11 = (f32[192]{0:T(256)S(1)}, f32[192]{0:T(256)}, u32[]{:S(2)}) copy-start(f32[192]{0:T(256)} %param.17) | copy-start | bytes 2308
  20.9 14.4 %copy-start.12 = (bf16[1,16,192]{2,1,0:T(8,128)(2,1)S(1)}, bf16[1,16,192]{2,1,0:T(8,128)(2,1)}, u32[]{:S(2)}) copy-start(bf16[1,16,192]{2,1,0:T(8,128)(2,1)} %param.14) | copy-start | bytes 18436
  20.9 14.8 %copy-start.6 = (bf16[192,192]{1,0:T(8,128)(2,1)S(1)}, bf16[192,192]{1,0:T(8,128)(2,1)}, u32[]{:S(2)}) copy-start(bf16[192,192]{1,0:T(8,128)(2,1)} %param.21) | copy-start | bytes 221188
  20.9 14.9 %copy-start.5 = (bf16[192,192]{1,0:T(8,128)(2,1)S(1)}, bf16[192,192]{1,0:T(8,128)(2,1)}, u32[]{:S(2)}) copy-start(bf16[192,192]{1,0:T(8,128)(2,1)} %param.22) | copy-start | bytes 221188
  24.6 10.7 %all-to-all-start.1 = ((bf16[8,2,192]{2,1,0:T(2,128)(2,1)}), bf16[8,2,192]{2,1,0:T(2,128)(2,1)S(1)}, u32[]{:S(2)}, u32[]{:S(2)}) async-start(bf16[8,2,192]{2,1,0:T(2,128)(2,1)} %copy.50), calls=%async_computation.1 | async-start | bytes 16384 | tf_op jit(solution)/shard_map/all_to_all | solution.py:75
  29.7 70.8 %reduce-scatter.7.cloned.1.call-start = ((), (), s32[]{:S(2)}) async-start(), calls=%async_computation.5 | async-start | bytes 73728
  69.4 2.3 copy-start.2
  71.7 60.3 %reduce-scatter.9.cloned.1.call-start = ((), (), s32[]{:S(2)}) async-start(), calls=%async_computation.6 | async-start | bytes 73728
  72.6 70.3 %copy-start.4 = (bf16[384,192]{0,1:T(8,128)(2,1)S(1)}, bf16[384,192]{0,1:T(8,128)(2,1)}, u32[]{:S(2)}) copy-start(bf16[384,192]{0,1:T(8,128)(2,1)} %param.19) | copy-start | bytes 442372
  72.6 70.4 %copy-start.10 = (f32[12,384]{1,0:T(8,128)S(1)}, f32[12,384]{1,0:T(8,128)}, u32[]{:S(2)}) copy-start(f32[12,384]{1,0:T(8,128)} %convert_reduce_fusion) | copy-start | bytes 55300
  133.8 8.9 %all-to-all-start.2 = ((bf16[8,2,192]{2,1,0:T(2,128)(2,1)}), bf16[8,2,192]{2,1,0:T(2,128)(2,1)S(1)}, u32[]{:S(2)}, u32[]{:S(2)}) async-start(bf16[8,2,192]{2,1,0:T(2,128)(2,1)} %reshape.172), calls=%async_computation.2 | async-start | bytes 16384 | tf_op jit(solution)/shard_map/all_to_all | solution.py:164
  137.1 106.9 %all-reduce.3.cloned.1.call-start = ((), (), s32[]{:S(2)}) async-start(), calls=%async_computation.7 | async-start | bytes 2752512 | tf_op jit(solution)/shard_map/psum | solution.py:186
  147.3 1.2 copy-start.7
  147.3 34.6 %copy-start.9 = (bf16[192,384]{1,0:T(8,128)(2,1)S(1)}, bf16[192,384]{1,0:T(8,128)(2,1)}, u32[]{:S(2)}) copy-start(bf16[192,384]{1,0:T(8,128)(2,1)} %param.18) | copy-start | bytes 442372
  244.0 8.4 %copy-start.8 = (f32[192,192]{1,0:T(8,128)S(1)}, f32[192,192]{1,0:T(8,128)}, u32[]{:S(2)}) copy-start(f32[192,192]{1,0:T(8,128)} %get-tuple-element.71) | copy-start | bytes 442372
Sparse Core Ops, SparseCore 0:
  71.8 28.6 reduce-scatter.6
  103.3 28.5 reduce-scatter.8
  148.7 95.3 all-reduce.2
where the time goes:
time: 260 us
  waiting for transfers between devices  126 us (48%)
  blocking collectives  60.4 us (23%)
  matrix products  25.1 us (10%)
  starting transfers between devices  14.9 us (6%)
  between operations  14 us (5%)
  local copies, waits for them, and re-layouts  13.3 us (5%)
  other arithmetic  6.46 us (2%)
    psum x1, waiting for transfers between devices, on_device(): lax.psum((grad_in, grad_out, grad_query, grad_key, grad_value, grad_proj,...  60.8 us
    unnamed x5, waiting for transfers between devices  57.2 us
    psum x1, blocking collectives, on_device(): lax.psum((grad_in, grad_out, grad_query, grad_key, grad_value, grad_proj,...  32.4 us
    all_gather x1, blocking collectives, on_device(): lax.all_gather(key_local, ('geom', 'head'), axis=0, tiled=True)  14 us
    all_gather x1, blocking collectives, on_device(): lax.all_gather(value_local, ('geom', 'head'), axis=0, tiled=True)  14 us
    unnamed x34, local copies, waits for them, and re-layouts  10.7 us
    dot_general x8, matrix products, contract_rows(): lax.dot_general(first_arg, second_arg, (((0,), (0,)), ((), ())), precisio...  7.61 us
    all_to_all x1, starting transfers between devices, on_device(): lax.all_to_all(slot_anchor.astype(jnp.float32).reshape(owners, CAP).astyp...  6.35 us
  transfers between devices with their start and end apart: 6, of which 5 were waited for; matrix products, arithmetic and copies ran while one was open for 7% of the time, Pallas kernels for 0%

commit v1 on v0

--- a/solution.py
+++ b/solution.py
@@ -183,9 +183,9 @@
     grad_out = contract_rows(hidden_sum, block_grad.astype(jnp.float32), exact_mode)
     grad_in = contract_rows(points, d_pre)
     d_input = times_transposed(d_pre, w_in).astype(jnp.bfloat16)
-    reduced = lax.psum(
-        (grad_in, grad_out, grad_query, grad_key, grad_value, grad_proj, grad_gain),
-        ("geom", "design", "head"),
+    _resolve_domain = lambda field_in: lax.psum(lax.psum(field_in, ("design", "head")), "geom")
+    reduced = _resolve_domain(
+        (grad_in, grad_out, grad_query, grad_key, grad_value, grad_proj, grad_gain)
     )
     return (
         attended[None],

time: 260 us -> 270 us (1.038)
  waiting for transfers between devices: 126 us -> 149 us
  blocking collectives: 60.4 us -> 46.8 us
    psum x1 -> x2, waiting for transfers between devices: 60.8 us -> 84.1 us  [the longest x1 44.7 us: on_device(): lax.psum(lax.psum(field_in, ('design', 'head')), 'geom')]
    psum x1 -> x2, blocking collectives: 32.4 us -> 18.8 us  [the longest x1 13.1 us: on_device(): lax.psum(lax.psum(field_in, ('design', 'head')), 'geom')]
    unnamed x5 -> x6, waiting for transfers between devices: 57.2 us -> 57.2 us
  transfers between devices with their start and end apart: 6 -> 7, of which waited for: 5 -> 6; matrix products, arithmetic and copies ran while one was open for 7% -> 6% of each run, Pallas kernels for 0% -> 0%
where the time goes in v1:
time: 270 us; the launch traced here: 269 us
  waiting for transfers between devices  149 us (55%)
  blocking collectives  46.8 us (17%)
  matrix products  25.1 us (9%)
  starting transfers between devices  14.9 us (6%)
  between operations  14 us (5%)
  local copies, waits for them, and re-layouts  13.3 us (5%)
  other arithmetic  6.46 us (2%)
    unnamed x6, waiting for transfers between devices  57.2 us
    psum x1, waiting for transfers between devices, on_device(): lax.psum(lax.psum(field_in, ('design', 'head')), 'geom')  44.7 us
    psum x1, waiting for transfers between devices, on_device(): lax.psum(field_in, ('design', 'head'))  39.4 us
    all_gather x1, blocking collectives, on_device(): lax.all_gather(key_local, ('geom', 'head'), axis=0, tiled=True)  14 us
    all_gather x1, blocking collectives, on_device(): lax.all_gather(value_local, ('geom', 'head'), axis=0, tiled=True)  14 us
    psum x1, blocking collectives, on_device(): lax.psum(lax.psum(field_in, ('design', 'head')), 'geom')  13.1 us
    unnamed x34, local copies, waits for them, and re-layouts  10.7 us
    dot_general x8, matrix products, contract_rows(): lax.dot_general(first_arg, second_arg, (((0,), (0,)), ((), ())), precisio...  7.61 us
  transfers between devices with their start and end apart: 7, of which 6 were waited for; matrix products, arithmetic and copies ran while one was open for 6% of the time, Pallas kernels for 0%

profile of v1, /device:TPU:0, one launch (start us, length us, event | category | flops | bytes accessed | tf_op | source)
XLA Modules:
  0.0 269.4 jit_solution(9408385870738555010)
XLA Ops:
  7.2 0.7 and_select_fusion
  7.9 0.7 add_bitcast_fusion
  8.6 0.2 convert_reduce_fusion.2
  8.8 0.1 select_reduce_fusion
  8.9 0.7 convert_element_type.190
  9.6 6.4 %all-to-all-start = ((bf16[8,1,2]{2,1,0:T(2,128)(2,1)}), bf16[8,1,2]{2,1,0:T(2,128)(2,1)S(1)}, u32[]{:S(2)}, u32[]{:S(2)}) async-start(bf16[8,1,2]{2,1,0:T(2,128)(2,1)} %convert_element_type.190), calls=%async_computation | async-start | bytes 8192 | tf_op jit(solution)/shard_map/all_to_all | solution.py:82
  16.0 3.2 %multiply_convert_fusion = (bf16[1536,384]{1,0:T(8,128)(2,1)S(1)}, f32[1536,384]{1,0:T(8,128)}) fusion(bf16[192,384]{1,0:T(8,128)(2,1)} %param.18, bf16[1,1536,192]{1,2,0:T(8,128)(2,1)S(1)} %copy-done), kind=kOutput, calls=%fused_computation.19 | convolution fusion | flops 231800832 | bytes 4276224 | tf_op jit(solution)/shard_map/dot_general | solution.py:69
  19.2 0.8 convert_reduce_fusion
  20.0 0.6 fusion.64
  20.6 0.2 reshape.166
  20.8 0.1 copy-done.1
  20.9 1.2 convolution_convert_fusion.5
  22.1 1.2 convolution_convert_fusion.1
  23.3 0.5 reduce_sum.95
  23.8 0.2 convolution_convert_fusion.12
  23.9 0.7 copy.50
  24.6 5.1 %all-to-all-start.1 = ((bf16[8,2,192]{2,1,0:T(2,128)(2,1)}), bf16[8,2,192]{2,1,0:T(2,128)(2,1)S(1)}, u32[]{:S(2)}, u32[]{:S(2)}) async-start(bf16[8,2,192]{2,1,0:T(2,128)(2,1)} %copy.50), calls=%async_computation.1 | async-start | bytes 16384 | tf_op jit(solution)/shard_map/all_to_all | solution.py:75
  29.8 0.1 convert_element_type.158
  29.9 0.1 convert_reduce_fusion.1
  30.0 5.3 %all-to-all-done.1 = bf16[8,2,192]{2,1,0:T(2,128)(2,1)S(1)} async-done(((bf16[8,2,192]{2,1,0:T(2,128)(2,1)}), bf16[8,2,192]{2,1,0:T(2,128)(2,1)S(1)}, u32[]{:S(2)}, u32[]{:S(2)}) %all-to-all-start.1) | async-done | bytes 6176 | tf_op jit(solution)/shard_map/all_to_all | solution.py:75
  35.4 0.2 multiply_reduce_fusion.3
  35.7 0.1 convolution_convert_fusion.10
  35.8 0.1 convolution_convert_fusion.11
  36.0 14.0 %all_gather.6 = bf16[128,192]{1,0:T(8,128)(2,1)S(1)} all-gather(bf16[16,192]{1,0:T(8,128)(2,1)S(1)} %convolution_convert_fusion.11), channel_id=1, replica_groups=mesh['groups'=2,'geom'=4,'design'=2,'head'=2] {'geom','head'}, dimensions={0}, use_global_device_ids=true | all-gather | bytes 55296 | tf_op jit(solution)/shard_map/all_gather | solution.py:102
  50.0 0.1 copy.51
  50.1 14.0 %all_gather.7 = bf16[128,192]{1,0:T(8,128)(2,1)S(1)} all-gather(bf16[16,192]{1,0:T(8,128)(2,1)S(1)} %convolution_convert_fusion.10), channel_id=1, replica_groups=mesh['groups'=2,'geom'=4,'design'=2,'head'=2] {'geom','head'}, dimensions={0}, use_global_device_ids=true | all-gather | bytes 55296 | tf_op jit(solution)/shard_map/all_gather | solution.py:101
  64.1 0.1 copy.52
  64.2 0.3 fusion.65
  64.5 1.3 fusion.63
  65.8 1.8 convolution_convert_fusion.7
  67.6 1.8 convolution_convert_fusion.2
  69.4 0.6 convolution_convert_fusion.4
  70.0 0.9 convolution_bitcast_fusion.1
  70.9 0.7 copy.64
  71.7 0.9 fusion.30
  72.6 0.6 convolution_convert_fusion.6
  73.2 0.7 copy.66
  74.0 26.5 %reduce-scatter.7.cloned.1.call-done = bf16[16,192]{1,0:T(8,128)(2,1)} async-done(((bf16[128,192]{1,0:T(8,128)(2,1)}), bf16[16,192]{1,0:T(8,128)(2,1)}) %reduce-scatter.7.cloned.1.call-update) | async-done | bytes 6160
  100.5 0.8 fusion.66
  101.4 30.6 %reduce-scatter.9.cloned.1.call-done = bf16[16,192]{1,0:T(8,128)(2,1)} async-done(((bf16[128,192]{1,0:T(8,128)(2,1)}), bf16[16,192]{1,0:T(8,128)(2,1)}) %reduce-scatter.9.cloned.1.call-update) | async-done | bytes 6160
  132.0 1.0 multiply_reduce_fusion.1
  133.0 0.2 convolution_convert_fusion.9
  133.2 0.6 reshape.172
  133.8 3.3 %all-to-all-start.2 = ((bf16[8,2,192]{2,1,0:T(2,128)(2,1)}), bf16[8,2,192]{2,1,0:T(2,128)(2,1)S(1)}, u32[]{:S(2)}, u32[]{:S(2)}) async-start(bf16[8,2,192]{2,1,0:T(2,128)(2,1)} %reshape.172), calls=%async_computation.2 | async-start | bytes 16384 | tf_op jit(solution)/shard_map/all_to_all | solution.py:164
  137.2 1.6 fusion.70
  138.8 1.6 fusion.69
  140.4 2.3 all-to-all-done.2
  142.7 0.2 convolution_convert_fusion.8
  142.9 0.1 fusion.67
  143.0 1.1 fusion.68
  144.1 3.2 %fusion.9 = bf16[1536,384]{1,0:T(8,128)(2,1)S(1)} fusion(f32[1536,384]{1,0:T(8,128)} %get-tuple-element.64, f32[12,384]{1,0:T(8,128)S(1)} %fusion.67), kind=kLoop, calls=%fused_computation.14 | loop fusion | flops 11796480 | bytes 3557376 | tf_op jit(solution)/shard_map/convert_element_type | solution.py:179
  147.4 1.2 convolution_bitcast_fusion
  148.6 39.4 %all-reduce.5.cloned.1.call-done = (f32[192,384]{1,0:T(8,128)}, f32[384,192]{0,1:T(8,128)}, f32[192,192]{0,1:T(8,128)}, f32[192,192]{1,0:T(8,128)}, f32[192,192]{1,0:T(8,128)}, /*index=5*/f32[192,192]{1,0:T(8,128)}) async-done(((f32[192,384]{1,0:T(8,128)}, f32[384,192]{0,1:T(8,128)}, f32[192,192]{0,1:T(8,128)}, f32[192,192]{1,0:T(8,128)}, f32[192,192]{1,0:T(8,128)}, /*index=5*/f32[192,192]{1,0:T(8,128)}), ...) | async-done | bytes 1179664 | tf_op jit(solution)/shard_map/psum | solution.py:186
  188.1 0.9 fusion.19
  189.0 5.7 %psum.110 = f32[192]{0:T(256)S(1)} all-reduce(f32[192]{0:T(256)S(1)} %get-tuple-element.45), channel_id=1, replica_groups=mesh['groups'=2,'geom'=4,'design'=2,'head'=2] {'design','head'}, use_global_device_ids=true, to_apply=%region_25.26 | all-reduce | flops 192 | bytes 1536 | tf_op jit(solution)/shard_map/psum | solution.py:186
  194.7 13.1 %psum.111 = f32[192]{0:T(256)} all-reduce(f32[192]{0:T(256)S(1)} %psum.110), channel_id=1, replica_groups=mesh['groups'=2,'geom'=4,'design'=2,'head'=2] {'geom'}, use_global_device_ids=true, to_apply=%region_26.27 | all-reduce | flops 192 | bytes 1536 | tf_op jit(solution)/shard_map/psum | solution.py:186
  207.8 1.4 fusion.2
  209.2 44.7 %all-reduce.7.cloned.1.call-done = (f32[192,384]{1,0:T(8,128)}, f32[384,192]{0,1:T(8,128)}, f32[192,192]{0,1:T(8,128)}, f32[192,192]{1,0:T(8,128)}, f32[192,192]{1,0:T(8,128)}, /*index=5*/f32[192,192]{1,0:T(8,128)}) async-done(((f32[192,384]{1,0:T(8,128)}, f32[384,192]{0,1:T(8,128)}, f32[192,192]{0,1:T(8,128)}, f32[192,192]{1,0:T(8,128)}, f32[192,192]{1,0:T(8,128)}, /*index=5*/f32[192,192]{1,0:T(8,128)}), ...) | async-done | bytes 1179664 | tf_op jit(solution)/shard_map/psum | solution.py:186
  253.8 1.8 copy.57
  255.6 1.7 copy.80
  257.3 1.7 copy.81
  259.0 1.6 copy.82
  260.6 1.6 copy.83
  262.2 0.7 copy.84
  (44 shorter events, 0.5 us)
Async XLA Ops:
  7.2 8.8 %copy-start = (bf16[1,1536,192]{1,2,0:T(8,128)(2,1)S(1)}, bf16[1,1536,192]{1,2,0:T(8,128)(2,1)}, u32[]{:S(2)}) copy-start(bf16[1,1536,192]{1,2,0:T(8,128)(2,1)} %param.12) | copy-start | bytes 1769476
  9.6 15.0 %all-to-all-start = ((bf16[8,1,2]{2,1,0:T(2,128)(2,1)}), bf16[8,1,2]{2,1,0:T(2,128)(2,1)S(1)}, u32[]{:S(2)}, u32[]{:S(2)}) async-start(bf16[8,1,2]{2,1,0:T(2,128)(2,1)} %convert_element_type.190), calls=%async_computation | async-start | bytes 8192 | tf_op jit(solution)/shard_map/all_to_all | solution.py:82
  16.0 4.0 %copy-start.3 = (bf16[384,192]{0,1:T(8,128)(2,1)S(1)}, bf16[384,192]{0,1:T(8,128)(2,1)}, u32[]{:S(2)}) copy-start(bf16[384,192]{0,1:T(8,128)(2,1)} %param.19) | copy-start | bytes 442372
  20.0 0.9 copy-start.1
  20.6 15.0 %copy-start.11 = (f32[192]{0:T(256)S(1)}, f32[192]{0:T(256)}, u32[]{:S(2)}) copy-start(f32[192]{0:T(256)} %param.17) | copy-start | bytes 2308
  20.9 14.4 %copy-start.12 = (bf16[1,16,192]{2,1,0:T(8,128)(2,1)S(1)}, bf16[1,16,192]{2,1,0:T(8,128)(2,1)}, u32[]{:S(2)}) copy-start(bf16[1,16,192]{2,1,0:T(8,128)(2,1)} %param.14) | copy-start | bytes 18436
  20.9 14.8 %copy-start.6 = (bf16[192,192]{1,0:T(8,128)(2,1)S(1)}, bf16[192,192]{1,0:T(8,128)(2,1)}, u32[]{:S(2)}) copy-start(bf16[192,192]{1,0:T(8,128)(2,1)} %param.21) | copy-start | bytes 221188
  20.9 14.9 %copy-start.5 = (bf16[192,192]{1,0:T(8,128)(2,1)S(1)}, bf16[192,192]{1,0:T(8,128)(2,1)}, u32[]{:S(2)}) copy-start(bf16[192,192]{1,0:T(8,128)(2,1)} %param.22) | copy-start | bytes 221188
  24.6 10.7 %all-to-all-start.1 = ((bf16[8,2,192]{2,1,0:T(2,128)(2,1)}), bf16[8,2,192]{2,1,0:T(2,128)(2,1)S(1)}, u32[]{:S(2)}, u32[]{:S(2)}) async-start(bf16[8,2,192]{2,1,0:T(2,128)(2,1)} %copy.50), calls=%async_computation.1 | async-start | bytes 16384 | tf_op jit(solution)/shard_map/all_to_all | solution.py:75
  29.7 70.8 %reduce-scatter.7.cloned.1.call-start = ((), (), s32[]{:S(2)}) async-start(), calls=%async_computation.5 | async-start | bytes 73728
  69.4 2.3 copy-start.2
  71.7 60.3 %reduce-scatter.9.cloned.1.call-start = ((), (), s32[]{:S(2)}) async-start(), calls=%async_computation.6 | async-start | bytes 73728
  72.6 70.3 %copy-start.4 = (bf16[384,192]{0,1:T(8,128)(2,1)S(1)}, bf16[384,192]{0,1:T(8,128)(2,1)}, u32[]{:S(2)}) copy-start(bf16[384,192]{0,1:T(8,128)(2,1)} %param.19) | copy-start | bytes 442372
  72.6 70.4 %copy-start.10 = (f32[12,384]{1,0:T(8,128)S(1)}, f32[12,384]{1,0:T(8,128)}, u32[]{:S(2)}) copy-start(f32[12,384]{1,0:T(8,128)} %convert_reduce_fusion) | copy-start | bytes 55300
  133.8 8.9 %all-to-all-start.2 = ((bf16[8,2,192]{2,1,0:T(2,128)(2,1)}), bf16[8,2,192]{2,1,0:T(2,128)(2,1)S(1)}, u32[]{:S(2)}, u32[]{:S(2)}) async-start(bf16[8,2,192]{2,1,0:T(2,128)(2,1)} %reshape.172), calls=%async_computation.2 | async-start | bytes 16384 | tf_op jit(solution)/shard_map/all_to_all | solution.py:164
  137.1 50.9 %all-reduce.5.cloned.1.call-start = ((), (), s32[]{:S(2)}) async-start(), calls=%async_computation.7 | async-start | bytes 2752512 | tf_op jit(solution)/shard_map/psum | solution.py:186
  147.3 40.7 %copy-start.7 = (bf16[192,192]{1,0:T(8,128)(2,1)S(1)}, bf16[192,192]{1,0:T(8,128)(2,1)}, u32[]{:S(2)}) copy-start(bf16[192,192]{1,0:T(8,128)(2,1)} %param.23) | copy-start | bytes 221188
  147.3 60.4 %copy-start.9 = (bf16[192,384]{1,0:T(8,128)(2,1)S(1)}, bf16[192,384]{1,0:T(8,128)(2,1)}, u32[]{:S(2)}) copy-start(bf16[192,384]{1,0:T(8,128)(2,1)} %param.18) | copy-start | bytes 442372
  148.6 105.3 %all-reduce.7.cloned.1.call-start = ((), (), s32[]{:S(2)}) async-start(), calls=%async_computation.8 | async-start | bytes 2752512 | tf_op jit(solution)/shard_map/psum | solution.py:186
  253.8 8.4 %copy-start.8 = (f32[192,192]{1,0:T(8,128)S(1)}, f32[192,192]{1,0:T(8,128)}, u32[]{:S(2)}) copy-start(f32[192,192]{1,0:T(8,128)} %get-tuple-element.77) | copy-start | bytes 442372
Sparse Core Ops, SparseCore 0:
  71.8 28.6 reduce-scatter.6
  103.3 28.5 reduce-scatter.8
  148.7 39.2 all-reduce.4
  190.7 63.0 all-reduce.6
